TPU v7x, 32 devices: a whole 2x2x4 slice. The times are simulated.
32 devices in a mesh: blk: 8 (over y, x, core), grp: 4 (over z).
Axes of the slice: x: 2, y: 2, z: 4, core: 2. Of those that a mesh axis runs over, the one named last changes fastest.
Arguments:
- amplitudes: bfloat16 [896, 4, 896], P('blk', None, 'grp'), may hold values from -6 to 6
- grid_factor: bfloat16 [1024, 896], P(('blk', 'grp')), may hold values from -0.1875 to 0.1875
- metric: float32 [1024, 4, 256], P('blk', 'grp'), may hold values from -6 to 6
- virt_energy: float32 [896], replicated, may hold values from 0.2 to 4
- pair_energy: float32 [4], replicated, may hold values from -2 to -0.5
Outputs:
- residual: float32 [896, 4, 896], P('blk', None, 'grp')
All inputs are finite; a program needn't handle non-finite values.
Results may differ from a plain program's by a relative error of at most 0.005.
Values may be sent and summed in bfloat16 or wider, within the bound.
A program may use at most 64 MiB of HBM per device.

v0:
```python
import jax
import jax.numpy as jnp
from jax import lax
from jax.sharding import PartitionSpec as P


def local(amplitudes, grid_factor, metric, virt_energy, pair_energy):
    row_factor = lax.all_gather(grid_factor, "grp", axis=0, tiled=True)
    column_factor = lax.all_gather(grid_factor, "blk", axis=0, tiled=True)
    amplitude_rows = lax.all_gather(amplitudes, "blk", axis=0, tiled=True)
    row_count = row_factor.shape[0]
    left_part = jnp.einsum(
        "pc,ckd->kpd", row_factor, amplitude_rows, preferred_element_type=jnp.float32
    ).astype(jnp.bfloat16)
    columns = column_factor
    products = jnp.einsum(
        "kpd,qd->kpq",
        lax.all_gather(left_part, "grp", axis=2, tiled=True),
        columns,
        preferred_element_type=jnp.float32,
    )
    weighted = (metric.reshape(row_count, -1)[None] * products).astype(jnp.bfloat16)
    columns = column_factor
    mixed = lax.psum_scatter(
        jnp.einsum("kpq,qb->bkp", weighted, columns, preferred_element_type=jnp.float32).astype(
            jnp.bfloat16
        ),
        "grp",
        scatter_dimension=0,
        tiled=True,
    )
    columns = row_factor
    ladder = lax.psum_scatter(
        jnp.einsum("pa,bkp->akb", columns, mixed, preferred_element_type=jnp.float32).astype(
            jnp.bfloat16
        ),
        "blk",
        scatter_dimension=0,
        tiled=True,
    ).astype(jnp.float32)
    first_energy = lax.dynamic_slice_in_dim(
        virt_energy, lax.axis_index("blk") * amplitudes.shape[0], amplitudes.shape[0]
    )
    second_energy = lax.dynamic_slice_in_dim(
        virt_energy, lax.axis_index("grp") * amplitudes.shape[2], amplitudes.shape[2]
    )
    denominator = (
        first_energy[:, None, None] + second_energy[None, None, :] - pair_energy[None, :, None]
    )
    return denominator * amplitudes.astype(jnp.float32) + ladder


def solution(mesh):
    in_specs = (P("blk", None, "grp"), P(("blk", "grp"), None), P("blk", "grp", None), P(), P())
    out_specs = P("blk", None, "grp")
    return jax.shard_map(local, mesh=mesh, in_specs=in_specs, out_specs=out_specs, check_vma=False)
```

profile of v0, /device:TPU:0, one launch (start us, length us, event | category | flops | bytes accessed | tf_op | source)
XLA Modules:
  0.0 138.9 jit_solution(9741608353748779387)
XLA Ops:
  6.5 0.0 all-gather.2.cloned.1.call-start
  6.5 0.7 all-gather.2.cloned.1.call-update
  7.3 0.0 reduce-scatter.5.cloned.1.call-start
  7.3 0.9 copy.23
  8.2 15.7 %all_gather.13 = bf16[128,896]{1,0:T(8,128)(2,1)S(1)} all-gather(bf16[32,896]{1,0:T(8,128)(2,1)} %param.6), channel_id=1, replica_groups=mesh['blk'=8,'grp'=4] {'grp'}, dimensions={0}, use_global_device_ids=true | all-gather | bytes 286720 | tf_op jit(solution)/shard_map/all_gather | solution.py:8
  24.0 11.1 %all_gather.15 = bf16[256,896]{1,0:T(8,128)(2,1)S(1)} all-gather(bf16[32,896]{1,0:T(8,128)(2,1)} %param.6), channel_id=1, replica_groups=mesh['blk'=8,'grp'=4] {'blk'}, dimensions={0}, use_global_device_ids=true | all-gather | bytes 516096 | tf_op jit(solution)/shard_map/all_gather | solution.py:9
  35.0 4.2 %all-gather.2.cloned.1.call-done = bf16[896,4,224]{2,1,0:T(4,128)(2,1)} async-done(((bf16[112,4,224]{2,1,0:T(4,128)(2,1)}), bf16[896,4,224]{2,1,0:T(4,128)(2,1)}) %all-gather.2.cloned.1.call-update) | async-done | bytes 1605648 | tf_op jit(solution)/shard_map/all_gather | solution.py:10
  39.3 2.2 %fusion.7 = bf16[4,128,224]{1,2,0:T(8,128)(2,1)S(1)} fusion(bf16[896,4,224]{2,1,0:T(4,128)(2,1)} %all-gather.2.cloned.1.call-done, bf16[128,896]{1,0:T(8,128)(2,1)S(1)} %all_gather.13), kind=kOutput, calls=%fused_computation.8 | convolution fusion | flops 205635584 | bytes 2064384 | tf_op jit(solution)/shard_map/pc,ckd->kpd/dot_general | solution.py:12
  41.5 21.0 %all_gather.14 = bf16[4,128,896]{1,2,0:T(8,128)(2,1)S(1)} all-gather(bf16[4,128,224]{1,2,0:T(8,128)(2,1)S(1)} %fusion.7), channel_id=1, replica_groups=mesh['blk'=8,'grp'=4] {'grp'}, dimensions={2}, use_global_device_ids=true | all-gather | bytes 1146880 | tf_op jit(solution)/shard_map/all_gather | solution.py:18
  62.5 2.2 %fusion.2 = bf16[896,4,128]{2,0,1:T(8,128)(2,1)} fusion(bf16[4,128,896]{1,2,0:T(8,128)(2,1)S(1)} %all_gather.14, bf16[256,896]{1,0:T(8,128)(2,1)S(1)} %all_gather.15, f32[128,256]{1,0:T(8,128)S(1)} %bitcast.25), kind=kOutput, calls=%fused_computation.4 | convolution fusion | flops 470482944 | bytes 2424832 | tf_op jit(solution)/shard_map/kpq,qb->bkp/dot_general | solution.py:25
  64.7 0.0 reduce-scatter.5.cloned.1.call-update
  64.7 0.0 reduce-scatter.7.cloned.1.call-start
  64.8 24.3 %reduce-scatter.5.cloned.1.call-done = bf16[224,4,128]{2,0,1:T(8,128)(2,1)} async-done(((bf16[896,4,128]{2,0,1:T(8,128)(2,1)}), bf16[224,4,128]{2,0,1:T(8,128)(2,1)}) %reduce-scatter.5.cloned.1.call-update) | async-done | bytes 229392 | tf_op jit(solution)/shard_map/reduce_scatter | solution.py:24
  89.1 1.5 %convolution_convert_fusion = bf16[224,4,896]{2,0,1:T(8,128)(2,1)S(1)} fusion(bf16[224,4,128]{2,0,1:T(8,128)(2,1)} %reduce-scatter.5.cloned.1.call-done, bf16[128,896]{1,0:T(8,128)(2,1)S(1)} %all_gather.13), kind=kOutput, calls=%fused_computation.2 | convolution fusion | flops 206323712 | bytes 2064384 | tf_op jit(solution)/shard_map/pa,bkp->akb/dot_general | solution.py:34
  90.6 0.0 copy-start
  90.6 2.3 %copy.13 = bf16[896,896]{1,0:T(8,128)(2,1)} copy(bf16[896,896]{0,1:T(8,128)(2,1)S(1)} %bitcast.23) | data formatting | bytes 3211264
  92.9 0.0 copy-start.1
  92.9 0.0 reduce-scatter.7.cloned.1.call-update
  92.9 0.0 copy-done
  93.0 0.2 copy.8
  93.2 0.8 dynamic_slice.7
  93.9 0.8 dynamic_slice.6
  94.7 0.1 broadcast_add_fusion
  94.8 35.4 %reduce-scatter.7.cloned.1.call-done = bf16[112,896]{1,0:T(8,128)(2,1)} async-done(((bf16[896,896]{1,0:T(8,128)(2,1)}), bf16[112,896]{1,0:T(8,128)(2,1)}) %reduce-scatter.7.cloned.1.call-update) | async-done | bytes 200720
  130.2 1.1 copy.14
  131.3 0.0 copy-done.1
  131.3 0.2 convert_add_fusion
  131.4 1.0 copy.9
Async XLA Ops:
  6.5 32.7 %all-gather.2.cloned.1.call-start = ((), (), s32[]{:S(2)}) async-start(), calls=%async_computation.2 | async-start | bytes 2064384 | tf_op jit(solution)/shard_map/all_gather | solution.py:10
  7.3 81.8 %reduce-scatter.5.cloned.1.call-start = ((), (), s32[]{:S(2)}) async-start(), calls=%async_computation.3 | async-start | bytes 1146880 | tf_op jit(solution)/shard_map/reduce_scatter | solution.py:24
  64.7 65.4 %reduce-scatter.7.cloned.1.call-start = ((), (), s32[]{:S(2)}) async-start(), calls=%async_computation.4 | async-start | bytes 1806336
  90.6 2.4 %copy-start = (bf16[112,4,224]{2,1,0:T(4,128)(2,1)S(1)}, bf16[112,4,224]{2,1,0:T(4,128)(2,1)}, u32[]{:S(2)}) copy-start(bf16[112,4,224]{2,1,0:T(4,128)(2,1)} %param.5) | copy-start | bytes 602116
  92.9 38.3 %copy-start.1 = (f32[4]{0:T(128)S(1)}, f32[4]{0:T(128)}, u32[]{:S(2)}) copy-start(f32[4]{0:T(128)} %param.9) | copy-start | bytes 52
Sparse Core Ops, SparseCore 0:
  9.2 30.0 all-gather.1
  64.8 24.2 reduce-scatter.4
  93.1 37.0 reduce-scatter.6
where the time goes:
time: 139 us
  waiting for transfers between devices  64.7 us (47%)
  blocking collectives  47.8 us (34%)
  between operations  13.2 us (9%)
  local copies, waits for them, and re-layouts  7.03 us (5%)
  matrix products  5.9 us (4%)
    unnamed x4, waiting for transfers between devices  36.1 us
    reduce_scatter x1, waiting for transfers between devices, local(): lax.psum_scatter(jnp.einsum('kpq,qb->bkp', weighted, columns, preferred_e...  24.3 us
    all_gather x1, blocking collectives, local(): lax.all_gather(left_part, 'grp', axis=2, tiled=True)  21 us
    all_gather x1, blocking collectives, local(): row_factor = lax.all_gather(grid_factor, 'grp', axis=0, tiled=True)  15.7 us
    all_gather x1, blocking collectives, local(): column_factor = lax.all_gather(grid_factor, 'blk', axis=0, tiled=True)  11.1 us
    unnamed x8, local copies, waits for them, and re-layouts  4.55 us
    all_gather x1, waiting for transfers between devices, local(): amplitude_rows = lax.all_gather(amplitudes, 'blk', axis=0, tiled=True)  4.22 us
  transfers between devices with their start and end apart: 3, of which 3 were waited for; matrix products, arithmetic and copies ran while one was open for 2% of the time, Pallas kernels for 0%

commit v1 on v0

--- a/solution.py
+++ b/solution.py
@@ -6,7 +6,22 @@
 
 def local(amplitudes, grid_factor, metric, virt_energy, pair_energy):
     row_factor = lax.all_gather(grid_factor, "grp", axis=0, tiled=True)
-    column_factor = lax.all_gather(grid_factor, "blk", axis=0, tiled=True)
+
+    def proceed_the_sources_all(base_x, mesh_name):
+        lanes = lax.axis_size(mesh_name)
+        built = sorted(((w, (w + 1) % lanes) for w in range(lanes)))
+        placed = base_x
+        bank = [placed]
+        it = 1
+        while it < lanes:
+            placed = lax.ppermute(placed, axis_name=mesh_name, perm=built)
+            bank.insert(0, placed)
+            it += 1
+        mat_out = jnp.concatenate(bank, axis=0)
+        val2 = lax.axis_index(mesh_name) + 1
+        return jnp.roll(mat_out, shift=val2 * base_x.shape[0], axis=0)
+
+    column_factor = proceed_the_sources_all(grid_factor, "blk")
     amplitude_rows = lax.all_gather(amplitudes, "blk", axis=0, tiled=True)
     row_count = row_factor.shape[0]
     left_part = jnp.einsum(

time: 139 us -> 152 us (1.094)
  waiting for transfers between devices: 64.7 us -> 89.9 us
  blocking collectives: 47.8 us -> 33.8 us
    ppermute x0 -> x7, waiting for transfers between devices: none -> 27.7 us  [proceed_the_sources_all(): placed = lax.ppermute(placed, axis_name=mesh_name, perm=built)]
    all_gather x1 -> x0, blocking collectives: 11.1 us -> none  [local(): column_factor = lax.all_gather(grid_factor, 'blk', axis=0, tiled=True)]
    all_gather x1, waiting for transfers between devices: 4.22 us -> 0.02 us  [local(): amplitude_rows = lax.all_gather(amplitudes, 'blk', axis=0, tiled=True)]
    all_gather x1, blocking collectives: 21 us -> 18.3 us  [local(): lax.all_gather(left_part, 'grp', axis=2, tiled=True)]
    reduce_scatter x1, waiting for transfers between devices: 24.3 us -> 26.1 us  [local(): lax.psum_scatter(jnp.einsum('kpq,qb->bkp', weighted, columns, preferred_e...]
    unnamed x8 -> x25, local copies, waits for them, and re-layouts: 4.55 us -> 5.58 us
  transfers between devices with their start and end apart: 3 -> 10, of which waited for: 3 -> 8; matrix products, arithmetic and copies ran while one was open for 2% -> 2% of each run, Pallas kernels for 0% -> 0%
where the time goes in v1:
time: 152 us
  waiting for transfers between devices  89.9 us (59%)
  blocking collectives  33.8 us (22%)
  between operations  13.3 us (9%)
  local copies, waits for them, and re-layouts  8.08 us (5%)
  matrix products  5.93 us (4%)
    unnamed x4, waiting for transfers between devices  36.1 us
    ppermute x7, waiting for transfers between devices, proceed_the_sources_all(): placed = lax.ppermute(placed, axis_name=mesh_name, perm=built)  27.7 us
    reduce_scatter x1, waiting for transfers between devices, local(): lax.psum_scatter(jnp.einsum('kpq,qb->bkp', weighted, columns, preferred_e...  26.1 us
    all_gather x1, blocking collectives, local(): lax.all_gather(left_part, 'grp', axis=2, tiled=True)  18.3 us
    all_gather x1, blocking collectives, local(): row_factor = lax.all_gather(grid_factor, 'grp', axis=0, tiled=True)  15.5 us
    unnamed x25, local copies, waits for them, and re-layouts  5.58 us
  transfers between devices with their start and end apart: 10, of which 8 were waited for; matrix products, arithmetic and copies ran while one was open for 2% of the time, Pallas kernels for 0%

profile of v1, /device:TPU:0, one launch (start us, length us, event | category | flops | bytes accessed | tf_op | source)
XLA Modules:
  0.0 151.8 jit_solution(14834468227192587217)
XLA Ops:
  6.5 0.0 copy-start.1
  6.5 0.0 all-gather.2.cloned.1.call-start
  6.5 0.7 all-gather.2.cloned.1.call-update
  7.3 0.0 reduce-scatter.5.cloned.1.call-start
  7.3 0.5 collective-permute-start
  7.8 4.9 %collective-permute-done = bf16[32,896]{1,0:T(8,128)(2,1)S(1)} collective-permute-done((bf16[32,896]{1,0:T(8,128)(2,1)}, bf16[32,896]{1,0:T(8,128)(2,1)S(1)}, u32[]{:S(2)}, u32[]{:S(2)}) %collective-permute-start) | collective-permute-done | bytes 57376 | tf_op jit(solution)/shard_map/ppermute | solution.py:17
  12.8 0.0 collective-permute-start.1
  12.8 4.5 %collective-permute-done.1 = bf16[32,896]{1,0:T(8,128)(2,1)S(1)} collective-permute-done((bf16[32,896]{1,0:T(8,128)(2,1)S(1)}, bf16[32,896]{1,0:T(8,128)(2,1)S(1)}, u32[]{:S(2)}, u32[]{:S(2)}) %collective-permute-start.1) | collective-permute-done | bytes 57376 | tf_op jit(solution)/shard_map/ppermute | solution.py:17
  17.3 0.0 collective-permute-start.2
  17.3 4.5 %collective-permute-done.2 = bf16[32,896]{1,0:T(8,128)(2,1)S(1)} collective-permute-done((bf16[32,896]{1,0:T(8,128)(2,1)S(1)}, bf16[32,896]{1,0:T(8,128)(2,1)S(1)}, u32[]{:S(2)}, u32[]{:S(2)}) %collective-permute-start.2) | collective-permute-done | bytes 57376 | tf_op jit(solution)/shard_map/ppermute | solution.py:17
  21.8 0.0 collective-permute-start.3
  21.8 4.5 %collective-permute-done.3 = bf16[32,896]{1,0:T(8,128)(2,1)S(1)} collective-permute-done((bf16[32,896]{1,0:T(8,128)(2,1)S(1)}, bf16[32,896]{1,0:T(8,128)(2,1)S(1)}, u32[]{:S(2)}, u32[]{:S(2)}) %collective-permute-start.3) | collective-permute-done | bytes 57376 | tf_op jit(solution)/shard_map/ppermute | solution.py:17
  26.3 0.0 collective-permute-start.4
  26.3 4.5 %collective-permute-done.4 = bf16[32,896]{1,0:T(8,128)(2,1)S(1)} collective-permute-done((bf16[32,896]{1,0:T(8,128)(2,1)S(1)}, bf16[32,896]{1,0:T(8,128)(2,1)S(1)}, u32[]{:S(2)}, u32[]{:S(2)}) %collective-permute-start.4) | collective-permute-done | bytes 57376 | tf_op jit(solution)/shard_map/ppermute | solution.py:17
  30.8 0.0 collective-permute-start.5
  30.8 0.9 copy.23
  31.7 4.8 %collective-permute-done.5 = bf16[32,896]{1,0:T(8,128)(2,1)S(1)} collective-permute-done((bf16[32,896]{1,0:T(8,128)(2,1)S(1)}, bf16[32,896]{1,0:T(8,128)(2,1)S(1)}, u32[]{:S(2)}, u32[]{:S(2)}) %collective-permute-start.5) | collective-permute-done | bytes 57376 | tf_op jit(solution)/shard_map/ppermute | solution.py:17
  36.5 0.0 collective-permute-start.6
  36.5 15.5 %all_gather.10 = bf16[128,896]{1,0:T(8,128)(2,1)S(1)} all-gather(bf16[32,896]{1,0:T(8,128)(2,1)} %param.6), channel_id=1, replica_groups=mesh['blk'=8,'grp'=4] {'grp'}, dimensions={0}, use_global_device_ids=true | all-gather | bytes 286720 | tf_op jit(solution)/shard_map/all_gather | solution.py:8
  52.0 0.0 collective-permute-done.6
  52.1 0.8 constant_dynamic-update-slice_fusion.8
  53.0 0.0 copy-done.1
  53.1 0.0 all-gather.2.cloned.1.call-done
  53.1 2.2 %fusion.6 = bf16[4,128,224]{1,2,0:T(8,128)(2,1)S(1)} fusion(bf16[896,4,224]{2,1,0:T(4,128)(2,1)} %all-gather.2.cloned.1.call-done, bf16[128,896]{1,0:T(8,128)(2,1)S(1)} %all_gather.10), kind=kOutput, calls=%fused_computation.7 | convolution fusion | flops 205635584 | bytes 2064384 | tf_op jit(solution)/shard_map/pc,ckd->kpd/dot_general | solution.py:27
  55.3 18.3 %all_gather.11 = bf16[4,128,896]{1,2,0:T(8,128)(2,1)S(1)} all-gather(bf16[4,128,224]{1,2,0:T(8,128)(2,1)S(1)} %fusion.6), channel_id=1, replica_groups=mesh['blk'=8,'grp'=4] {'grp'}, dimensions={2}, use_global_device_ids=true | all-gather | bytes 1146880 | tf_op jit(solution)/shard_map/all_gather | solution.py:33
  73.7 2.2 %convolution_convert_fusion.1 = bf16[896,4,128]{2,0,1:T(8,128)(2,1)} fusion(bf16[4,128,896]{1,2,0:T(8,128)(2,1)S(1)} %all_gather.11, bf16[512,896]{1,0:T(8,128)(2,1)S(1)} %constant_dynamic-update-slice_fusion, s32[]{:T(128)S(6)} %select_n.22, f32[128,256]{1,0:T(8,128)S(1)} %bitcast.23), kind=kOutput, calls=%fused_computation.3 | convolution fusion | flops 470482944 | bytes 2884608 | tf_op jit(solution)/shard_map/kpq,qb->bkp/dot_general | solution.py:40
  75.9 0.0 reduce-scatter.5.cloned.1.call-update
  75.9 0.0 reduce-scatter.7.cloned.1.call-start
  75.9 26.1 %reduce-scatter.5.cloned.1.call-done = bf16[224,4,128]{2,0,1:T(8,128)(2,1)} async-done(((bf16[896,4,128]{2,0,1:T(8,128)(2,1)}), bf16[224,4,128]{2,0,1:T(8,128)(2,1)}) %reduce-scatter.5.cloned.1.call-update) | async-done | bytes 229392 | tf_op jit(solution)/shard_map/reduce_scatter | solution.py:39
  102.0 1.5 convolution_convert_fusion
  103.5 0.0 copy-start
  103.5 2.3 %copy.13 = bf16[896,896]{1,0:T(8,128)(2,1)} copy(bf16[896,896]{0,1:T(8,128)(2,1)S(1)} %bitcast.21) | data formatting | bytes 3211264
  105.8 0.0 copy-start.2
  105.8 0.0 reduce-scatter.7.cloned.1.call-update
  105.9 0.0 copy-done
  105.9 0.2 copy.8
  106.1 0.8 dynamic_slice.10
  106.9 0.8 dynamic_slice.11
  107.6 0.1 broadcast_add_fusion
  107.7 35.3 %reduce-scatter.7.cloned.1.call-done = bf16[112,896]{1,0:T(8,128)(2,1)} async-done(((bf16[896,896]{1,0:T(8,128)(2,1)}), bf16[112,896]{1,0:T(8,128)(2,1)}) %reduce-scatter.7.cloned.1.call-update) | async-done | bytes 200720
  143.1 1.1 copy.14
  144.2 0.0 copy-done.2
  144.2 0.2 convert_add_fusion
  144.3 1.0 copy.9
  (15 shorter events, 0.2 us)
Async XLA Ops:
  6.5 46.5 %copy-start.1 = (bf16[32,896]{1,0:T(8,128)(2,1)S(1)}, bf16[32,896]{1,0:T(8,128)(2,1)}, u32[]{:S(2)}) copy-start(bf16[32,896]{1,0:T(8,128)(2,1)} %param.6) | copy-start | bytes 172036
  6.5 46.5 %all-gather.2.cloned.1.call-start = ((), (), s32[]{:S(2)}) async-start(), calls=%async_computation.2 | async-start | bytes 2064384 | tf_op jit(solution)/shard_map/all_gather | solution.py:25
  7.3 94.7 %reduce-scatter.5.cloned.1.call-start = ((), (), s32[]{:S(2)}) async-start(), calls=%async_computation.3 | async-start | bytes 1146880 | tf_op jit(solution)/shard_map/reduce_scatter | solution.py:39
  7.3 5.5 %collective-permute-start = (bf16[32,896]{1,0:T(8,128)(2,1)}, bf16[32,896]{1,0:T(8,128)(2,1)S(1)}, u32[]{:S(2)}, u32[]{:S(2)}) collective-permute-start(bf16[32,896]{1,0:T(8,128)(2,1)} %param.6), channel_id=1, source_target_pairs={{0,4},{4,8},{8,12},{12,16},{16,20},{20,24},{24,28},{28,0},{1,5},{5... | collective-permute-start | bytes 172040 | tf_op jit(solution)/shard_map/ppermute | solution.py:17
  12.8 4.5 %collective-permute-start.1 = (bf16[32,896]{1,0:T(8,128)(2,1)S(1)}, bf16[32,896]{1,0:T(8,128)(2,1)S(1)}, u32[]{:S(2)}, u32[]{:S(2)}) collective-permute-start(bf16[32,896]{1,0:T(8,128)(2,1)S(1)} %collective-permute-done), channel_id=1, source_target_pairs={{0,4},{4,8},{8,12},{12,16},{16,20},{20,24},{24,28},{28,0},{1,5},{5... | collective-permute-start | bytes 172040 | tf_op jit(solution)/shard_map/ppermute | solution.py:17
  17.3 4.5 %collective-permute-start.2 = (bf16[32,896]{1,0:T(8,128)(2,1)S(1)}, bf16[32,896]{1,0:T(8,128)(2,1)S(1)}, u32[]{:S(2)}, u32[]{:S(2)}) collective-permute-start(bf16[32,896]{1,0:T(8,128)(2,1)S(1)} %collective-permute-done.1), channel_id=1, source_target_pairs={{0,4},{4,8},{8,12},{12,16},{16,20},{20,24},{24,28},{28,0},{1,5},{5... | collective-permute-start | bytes 172040 | tf_op jit(solution)/shard_map/ppermute | solution.py:17
  21.8 4.5 %collective-permute-start.3 = (bf16[32,896]{1,0:T(8,128)(2,1)S(1)}, bf16[32,896]{1,0:T(8,128)(2,1)S(1)}, u32[]{:S(2)}, u32[]{:S(2)}) collective-permute-start(bf16[32,896]{1,0:T(8,128)(2,1)S(1)} %collective-permute-done.2), channel_id=1, source_target_pairs={{0,4},{4,8},{8,12},{12,16},{16,20},{20,24},{24,28},{28,0},{1,5},{5... | collective-permute-start | bytes 172040 | tf_op jit(solution)/shard_map/ppermute | solution.py:17
  26.3 4.5 %collective-permute-start.4 = (bf16[32,896]{1,0:T(8,128)(2,1)S(1)}, bf16[32,896]{1,0:T(8,128)(2,1)S(1)}, u32[]{:S(2)}, u32[]{:S(2)}) collective-permute-start(bf16[32,896]{1,0:T(8,128)(2,1)S(1)} %collective-permute-done.3), channel_id=1, source_target_pairs={{0,4},{4,8},{8,12},{12,16},{16,20},{20,24},{24,28},{28,0},{1,5},{5... | collective-permute-start | bytes 172040 | tf_op jit(solution)/shard_map/ppermute | solution.py:17
  30.8 5.7 %collective-permute-start.5 = (bf16[32,896]{1,0:T(8,128)(2,1)S(1)}, bf16[32,896]{1,0:T(8,128)(2,1)S(1)}, u32[]{:S(2)}, u32[]{:S(2)}) collective-permute-start(bf16[32,896]{1,0:T(8,128)(2,1)S(1)} %collective-permute-done.4), channel_id=1, source_target_pairs={{0,4},{4,8},{8,12},{12,16},{16,20},{20,24},{24,28},{28,0},{1,5},{5... | collective-permute-start | bytes 172040 | tf_op jit(solution)/shard_map/ppermute | solution.py:17
  36.5 15.5 %collective-permute-start.6 = (bf16[32,896]{1,0:T(8,128)(2,1)S(1)}, bf16[32,896]{1,0:T(8,128)(2,1)S(1)}, u32[]{:S(2)}, u32[]{:S(2)}) collective-permute-start(bf16[32,896]{1,0:T(8,128)(2,1)S(1)} %collective-permute-done.5), channel_id=1, source_target_pairs={{0,4},{4,8},{8,12},{12,16},{16,20},{20,24},{24,28},{28,0},{1,5},{5... | collective-permute-start | bytes 172040 | tf_op jit(solution)/shard_map/ppermute | solution.py:17
  75.9 67.2 %reduce-scatter.7.cloned.1.call-start = ((), (), s32[]{:S(2)}) async-start(), calls=%async_computation.4 | async-start | bytes 1806336
  103.5 2.4 %copy-start = (bf16[112,4,224]{2,1,0:T(4,128)(2,1)S(1)}, bf16[112,4,224]{2,1,0:T(4,128)(2,1)}, u32[]{:S(2)}) copy-start(bf16[112,4,224]{2,1,0:T(4,128)(2,1)} %param.5) | copy-start | bytes 602116
  105.8 38.3 %copy-start.2 = (f32[4]{0:T(128)S(1)}, f32[4]{0:T(128)}, u32[]{:S(2)}) copy-start(f32[4]{0:T(128)} %param.9) | copy-start | bytes 52
Sparse Core Ops, SparseCore 0:
  9.2 30.1 all-gather.1
  76.0 25.9 reduce-scatter.4
  106.0 37.0 reduce-scatter.6
